TPU v7x, 32 devices: a whole 2x2x4 slice. The times are simulated.
32 devices in a mesh: tp: 8 (over z, y), dp: 4 (over x, core).
Axes of the slice: x: 2, y: 2, z: 4, core: 2. Of those that a mesh axis runs over, the one named last changes fastest.
Arguments:
- tokens: bfloat16 [768, 4096], P(('dp', 'tp')), may hold values from -6 to 6
- hidden_grad: bfloat16 [768, 14336], P('dp', 'tp'), may hold values from -0.59765625 to 0.59765625
- gate_value: bfloat16 [768, 14336], P('dp', 'tp'), may hold values from -6 to 6
- up_value: bfloat16 [768, 14336], P('dp', 'tp'), may hold values from -6 to 6
- gate_weight: bfloat16 [4096, 14336], P('dp', 'tp'), may hold values from -0.09375 to 0.09375
- up_weight: bfloat16 [4096, 14336], P('dp', 'tp'), may hold values from -0.09375 to 0.09375
Outputs:
- input_grad: bfloat16 [768, 4096], P(('dp', 'tp'))
- gate_grad: bfloat16 [4096, 14336], P('dp', 'tp')
- up_grad: bfloat16 [4096, 14336], P('dp', 'tp')
All inputs are finite; a program needn't handle non-finite values.
Results may differ from a plain program's by a relative error of at most 0.018.
Values may be sent and summed in bfloat16 or wider, within the bound.
A program may use at most 128 MiB of HBM per device.

v0:
```python
import jax
import jax.numpy as jnp
from jax import lax
from jax.sharding import PartitionSpec as P


def on_device(tokens, hidden_grad, gate_value, up_value, gate_weight, up_weight):
    gathered = lax.all_gather(tokens, "tp", axis=0, tiled=True)
    gate_full, up_full = (
        lax.all_gather(gate_weight, "dp", axis=0, tiled=True),
        lax.all_gather(up_weight, "dp", axis=0, tiled=True),
    )
    gate_float = gate_value.astype(jnp.float32)
    up_float = up_value.astype(jnp.float32)
    logistic = jax.nn.sigmoid(gate_float)
    upstream = hidden_grad.astype(jnp.float32)
    d_gate = (upstream * up_float * logistic * (1.0 + gate_float * (1.0 - logistic))).astype(
        jnp.bfloat16
    )
    d_up = (upstream * gate_float * logistic).astype(jnp.bfloat16)
    across = (((1,), (1,)), ((), ()))
    contract = (((0,), (0,)), ((), ()))
    input_grad = lax.psum_scatter(
        (
            lax.dot_general(d_gate, gate_full, across, preferred_element_type=jnp.float32)
            + lax.dot_general(d_up, up_full, across, preferred_element_type=jnp.float32)
        ).astype(jnp.bfloat16),
        "tp",
        scatter_dimension=0,
        tiled=True,
    )
    grads_both = jnp.concatenate([d_gate, d_up], axis=1)
    hidden_width = d_gate.shape[1]
    group_rows = gathered.shape[0]
    columns = lax.all_to_all(gathered, "dp", split_axis=1, concat_axis=0, tiled=True)
    initial = jnp.zeros((gate_weight.shape[0], 2 * hidden_width), jnp.float32)
    pieces = lax.all_gather(grads_both, "dp", axis=0, tiled=True)
    group_count = pieces.shape[0] // group_rows

    def one_group(position, carried):
        within = position * group_rows
        grads_rows = lax.dynamic_slice_in_dim(pieces, within, group_rows, 0)
        block = lax.dynamic_slice_in_dim(columns, within, group_rows, 0)
        partial_value = lax.dot_general(
            block, grads_rows, contract, preferred_element_type=jnp.float32
        ).astype(jnp.bfloat16)
        partial_value = lax.optimization_barrier(partial_value)
        return carried + partial_value.astype(jnp.float32)

    summed = lax.fori_loop(0, group_count, one_group, initial)
    gate_grad = summed[:, :hidden_width].astype(jnp.bfloat16)
    up_grad = summed[:, hidden_width:].astype(jnp.bfloat16)
    return (input_grad, gate_grad, up_grad)


def solution(mesh):
    placed = (
        P(("dp", "tp"), None),
        P("dp", "tp"),
        P("dp", "tp"),
        P("dp", "tp"),
        P("dp", "tp"),
        P("dp", "tp"),
    )
    return jax.shard_map(
        on_device,
        mesh=mesh,
        in_specs=placed,
        out_specs=(P(("dp", "tp"), None), P("dp", "tp"), P("dp", "tp")),
        check_vma=False,
    )
```

profile of v0, /device:TPU:0, one launch (start us, length us, event | category | flops | bytes accessed | tf_op | source)
XLA Modules:
  0.0 376.7 jit_solution(9638341866954031148)
XLA Ops:
  7.2 0.0 all-gather.9.cloned.1.call-start
  7.2 0.7 all-gather.9.cloned.1.call-update
  7.9 0.0 copy-start
  7.9 0.0 copy-start.1
  7.9 0.0 all-gather.5.cloned.1.call-start
  8.0 0.7 all-gather.5.cloned.1.call-update
  8.7 0.0 all-gather.7.cloned.1.call-start
  8.7 0.7 all-gather.7.cloned.1.call-update
  9.4 0.0 all-gather.11.cloned.1.call-start
  9.4 0.0 copy-done
  9.5 0.0 copy-done.1
  9.5 1.8 fusion.12
  11.3 1.2 pad_maximum_fusion
  12.5 0.0 all-gather.11.cloned.1.call-update
  12.5 44.6 %all-gather.9.cloned.1.call-done = bf16[192,4096]{1,0:T(8,128)(2,1)} async-done(((bf16[24,4096]{1,0:T(8,128)(2,1)}), bf16[192,4096]{1,0:T(8,128)(2,1)}) %all-gather.9.cloned.1.call-update) | async-done | bytes 1572880 | tf_op jit(solution)/shard_map/all_gather | solution.py:8
  57.1 2.7 copy.12
  59.8 3.6 all-to-all-start
  63.4 0.0 reduce-scatter.2.cloned.1.call-start
  63.4 100.7 %all-gather.5.cloned.1.call-done = bf16[4096,1792]{1,0:T(8,128)(2,1)} async-done(((bf16[1024,1792]{1,0:T(8,128)(2,1)}), bf16[4096,1792]{1,0:T(8,128)(2,1)}) %all-gather.5.cloned.1.call-update) | async-done | bytes 14680080 | tf_op jit(solution)/shard_map/all_gather | solution.py:10
  164.1 11.9 %fusion.14 = f32[192,4096]{1,0:T(8,128)} fusion(bf16[192,1792]{1,0:T(8,128)(2,1)S(1)} %get-tuple-element.109, bf16[4096,1792]{1,0:T(8,128)(2,1)} %all-gather.5.cloned.1.call-done), kind=kOutput, calls=%fused_computation.23 | convolution fusion | flops 2818572288 | bytes 18513920 | tf_op jit(solution)/shard_map/dot_general | solution.py:25
  176.0 81.2 %all-gather.7.cloned.1.call-done = bf16[4096,1792]{1,0:T(8,128)(2,1)} async-done(((bf16[1024,1792]{1,0:T(8,128)(2,1)}), bf16[4096,1792]{1,0:T(8,128)(2,1)}) %all-gather.7.cloned.1.call-update) | async-done | bytes 14680080 | tf_op jit(solution)/shard_map/all_gather | solution.py:11
  257.1 12.1 %fusion.3 = bf16[192,4096]{1,0:T(8,128)(2,1)} fusion(f32[192,4096]{1,0:T(8,128)} %fusion.14, bf16[192,1792]{1,0:T(8,128)(2,1)S(1)} %get-tuple-element.108, bf16[4096,1792]{1,0:T(8,128)(2,1)} %all-gather.7.cloned.1.call-done), kind=kOutput, calls=%fused_computation.6 | convolution fusion | flops 2820145152 | bytes 20086784 | tf_op jit(solution)/shard_map/dot_general | solution.py:26
  269.3 0.0 reduce-scatter.2.cloned.1.call-update
  269.3 0.0 all-to-all-done
  269.3 31.2 %all-gather.11.cloned.1.call-done = bf16[768,3584]{1,0:T(8,128)(2,1)} async-done(((bf16[192,3584]{1,0:T(8,128)(2,1)}), bf16[768,3584]{1,0:T(8,128)(2,1)}) %all-gather.11.cloned.1.call-update) | async-done | bytes 5505040 | tf_op jit(solution)/shard_map/all_gather | solution.py:37
  300.5 52.8 %while.14 = (s32[]{:T(128)}, f32[1024,3584]{1,0:T(8,128)}, bf16[768,1024]{1,0:T(8,128)(2,1)S(1)}, bf16[768,3584]{1,0:T(8,128)(2,1)}, s32[]{:T(128)}, /*index=5*/s32[]{:T(128)}, s32[]{:T(128)}, s32[]{:T(128)}) while((s32[]{:T(128)}, f32[1024,3584]{1,0:T(8,128)}, bf16[768,1024]{1,0:T(8,128)(2,1)S(1)}, bf16[768,3584]{1,0:T(8,128)(2,1)}, ...), condition=%wide.region_2.0_spmd.clone, body=%wide.region_1.0_spmd.clone.sunk | while | flops 1423966208 | bytes 45810836 | solution.py:50
  300.5 3.5 convolution_convert_fusion.2
  304.0 5.9 %select_add_fusion.2 = f32[1024,3584]{1,0:T(8,128)} fusion(f32[1024,3584]{1,0:T(8,128)} %get-tuple-element.144, bf16[1024,3584]{1,0:T(8,128)(2,1)S(1)} %convolution_convert_fusion.2, pred[]{:T(512)S(6)} %compare.3), kind=kLoop, calls=%fused_computation.clone.1 | loop fusion | flops 11010048 | bytes 36700160 | tf_op jit(solution)/shard_map/while/body/eval_jaxpr/add | solution.py:48
  309.9 3.4 convolution_convert_fusion.2
  313.4 11.0 %select_add_fusion.2 = f32[1024,3584]{1,0:T(8,128)} fusion(f32[1024,3584]{1,0:T(8,128)} %get-tuple-element.144, bf16[1024,3584]{1,0:T(8,128)(2,1)S(1)} %convolution_convert_fusion.2, pred[]{:T(512)S(6)} %compare.3), kind=kLoop, calls=%fused_computation.clone.1 | loop fusion | flops 11010048 | bytes 36700160 | tf_op jit(solution)/shard_map/while/body/eval_jaxpr/add | solution.py:48
  324.4 3.5 convolution_convert_fusion.2
  327.9 11.0 %select_add_fusion.2 = f32[1024,3584]{1,0:T(8,128)} fusion(f32[1024,3584]{1,0:T(8,128)} %get-tuple-element.144, bf16[1024,3584]{1,0:T(8,128)(2,1)S(1)} %convolution_convert_fusion.2, pred[]{:T(512)S(6)} %compare.3), kind=kLoop, calls=%fused_computation.clone.1 | loop fusion | flops 11010048 | bytes 36700160 | tf_op jit(solution)/shard_map/while/body/eval_jaxpr/add | solution.py:48
  338.9 3.4 convolution_convert_fusion.2
  342.3 11.0 %select_add_fusion.2 = f32[1024,3584]{1,0:T(8,128)} fusion(f32[1024,3584]{1,0:T(8,128)} %get-tuple-element.144, bf16[1024,3584]{1,0:T(8,128)(2,1)S(1)} %convolution_convert_fusion.2, pred[]{:T(512)S(6)} %compare.3), kind=kLoop, calls=%fused_computation.clone.1 | loop fusion | flops 11010048 | bytes 36700160 | tf_op jit(solution)/shard_map/while/body/eval_jaxpr/add | solution.py:48
  353.3 9.1 %convert.4 = bf16[1024,3584]{1,0:T(8,128)(2,1)} convert(f32[1024,3584]{1,0:T(8,128)} %get-tuple-element.82) | non-fusion elementwise | flops 3670016 | bytes 22020096 | tf_op jit(solution)/shard_map/convert.1
  362.4 6.7 %fusion.13 = (bf16[1024,1792]{1,0:T(8,128)(2,1)}, bf16[1024,1792]{1,0:T(8,128)(2,1)}) fusion(bf16[1024,3584]{1,0:T(8,128)(2,1)} %convert.4), kind=kLoop, calls=%fused_computation.22 | loop fusion | bytes 14680064 | tf_op jit(solution)/shard_map/slice | solution.py:52
  369.1 1.0 reduce-scatter.2.cloned.1.call-done
  (1 shorter events, 0.0 us)
Async XLA Ops:
  7.2 49.9 %all-gather.9.cloned.1.call-start = ((), (), s32[]{:S(2)}) async-start(), calls=%async_computation.5 | async-start | bytes 1769472 | tf_op jit(solution)/shard_map/all_gather | solution.py:8
  7.9 1.6 copy-start
  7.9 1.6 copy-start.1
  7.9 156.2 %all-gather.5.cloned.1.call-start = ((), (), s32[]{:S(2)}) async-start(), calls=%async_computation.2 | async-start | bytes 18350080 | tf_op jit(solution)/shard_map/all_gather | solution.py:10
  8.7 248.5 %all-gather.7.cloned.1.call-start = ((), (), s32[]{:S(2)}) async-start(), calls=%async_computation.3 | async-start | bytes 18350080 | tf_op jit(solution)/shard_map/all_gather | solution.py:11
  9.4 291.1 %all-gather.11.cloned.1.call-start = ((), (), s32[]{:S(2)}) async-start(), calls=%async_computation.6 | async-start | bytes 6881280 | tf_op jit(solution)/shard_map/all_gather | solution.py:37
  59.8 209.5 %all-to-all-start = ((bf16[192,4,1024]{2,0,1:T(8,128)(2,1)}), bf16[192,4,1024]{2,0,1:T(8,128)(2,1)S(1)}, u32[]{:S(2)}, u32[]{:S(2)}) async-start(bf16[192,4,1024]{2,0,1:T(8,128)(2,1)} %bitcast.10), calls=%async_computation.1 | async-start | bytes 3145728 | tf_op jit(solution)/shard_map/all_to_all | solution.py:35
  63.4 306.8 %reduce-scatter.2.cloned.1.call-start = ((), (), s32[]{:S(2)}) async-start(), calls=%async_computation.4 | async-start | bytes 1769472 | tf_op jit(solution)/shard_map/reduce_scatter | solution.py:23
Sparse Core Ops, SparseCore 0:
  10.2 46.8 all-gather.8
  58.6 105.4 all-gather.4
  165.7 91.4 all-gather.6
  258.6 41.8 all-gather.10
  304.3 65.7 reduce-scatter.1
where the time goes:
time: 377 us
  waiting for transfers between devices  261 us (69%)
  other arithmetic  51.1 us (14%)
  matrix products  37.9 us (10%)
  between operations  13.8 us (4%)
  local copies, waits for them, and re-layouts  9.4 us (2%)
    all_gather x1, waiting for transfers between devices, on_device(): lax.all_gather(gate_weight, 'dp', axis=0, tiled=True)  101 us
    all_gather x1, waiting for transfers between devices, on_device(): lax.all_gather(up_weight, 'dp', axis=0, tiled=True)  81.2 us
    all_gather x1, waiting for transfers between devices, on_device(): gathered = lax.all_gather(tokens, 'tp', axis=0, tiled=True)  44.6 us
    add x4, other arithmetic, one_group(): return carried + partial_value.astype(jnp.float32)  39 us
    all_gather x1, waiting for transfers between devices, on_device(): pieces = lax.all_gather(grads_both, 'dp', axis=0, tiled=True)  31.2 us
    dot_general x4, matrix products, one_group(): lax.dot_general(block, grads_rows, contract, preferred_element_type=jnp.f...  13.8 us
    dot_general x1, matrix products, on_device(): lax.dot_general(d_up, up_full, across, preferred_element_type=jnp.float32)  12.1 us
    dot_general x1, matrix products, on_device(): lax.dot_general(d_gate, gate_full, across, preferred_element_type=jnp.flo...  11.9 us
  transfers between devices with their start and end apart: 6, of which 5 were waited for; matrix products, arithmetic and copies ran while one was open for 26% of the time, Pallas kernels for 0%

commit v1 on v0

--- a/solution.py
+++ b/solution.py
@@ -34,7 +34,14 @@
     group_rows = gathered.shape[0]
     columns = lax.all_to_all(gathered, "dp", split_axis=1, concat_axis=0, tiled=True)
     initial = jnp.zeros((gate_weight.shape[0], 2 * hidden_width), jnp.float32)
-    pieces = lax.all_gather(grads_both, "dp", axis=0, tiled=True)
+    peers = lax.axis_size("dp")
+    hops = [(i, (i + 1) % peers) for i in range(peers)]
+    parts = [grads_both]
+    for reach in range(1, peers):
+        parts = [lax.ppermute(parts[0], "dp", hops), *parts]
+    whole = jnp.concatenate(parts, axis=0)
+    turn = (lax.axis_index("dp") + 1) * parts[-1].shape[0]
+    pieces = jnp.roll(whole, turn, axis=0)
     group_count = pieces.shape[0] // group_rows
 
     def one_group(position, carried):

time: 377 us -> 350 us (0.928)
  waiting for transfers between devices: 261 us -> 222 us
  local copies, waits for them, and re-layouts: 9.4 us -> 21.1 us
    ppermute x0 -> x3, waiting for transfers between devices: none -> 39.1 us  [on_device(): parts = [lax.ppermute(parts[0], 'dp', hops), *parts]]
    all_gather x1, waiting for transfers between devices: 44.6 us -> 8.33 us  [on_device(): gathered = lax.all_gather(tokens, 'tp', axis=0, tiled=True)]
    all_gather x1 -> x0, waiting for transfers between devices: 31.2 us -> none  [on_device(): pieces = lax.all_gather(grads_both, 'dp', axis=0, tiled=True)]
    all_gather x1, waiting for transfers between devices: 101 us -> 86.7 us  [on_device(): lax.all_gather(gate_weight, 'dp', axis=0, tiled=True)]
    unnamed x4 -> x14, local copies, waits for them, and re-layouts: 0.01 us -> 7.95 us
    all_gather x1, waiting for transfers between devices: 81.2 us -> 85.9 us  [on_device(): lax.all_gather(up_weight, 'dp', axis=0, tiled=True)]
  transfers between devices with their start and end apart: 6 -> 8, of which waited for: 5 -> 6; matrix products, arithmetic and copies ran while one was open for 26% -> 31% of each run, Pallas kernels for 0% -> 0%
where the time goes in v1:
time: 350 us; the launch traced here: 349 us
  waiting for transfers between devices  222 us (63%)
  other arithmetic  49.8 us (14%)
  matrix products  37.7 us (11%)
  local copies, waits for them, and re-layouts  21.1 us (6%)
  between operations  13.9 us (4%)
  starting transfers between devices  4.27 us (1%)
    all_gather x1, waiting for transfers between devices, on_device(): lax.all_gather(gate_weight, 'dp', axis=0, tiled=True)  86.7 us
    all_gather x1, waiting for transfers between devices, on_device(): lax.all_gather(up_weight, 'dp', axis=0, tiled=True)  85.9 us
    ppermute x3, waiting for transfers between devices, on_device(): parts = [lax.ppermute(parts[0], 'dp', hops), *parts]  39.1 us
    add x4, other arithmetic, one_group(): return carried + partial_value.astype(jnp.float32)  38.7 us
    dot_general x4, matrix products, one_group(): lax.dot_general(block, grads_rows, contract, preferred_element_type=jnp.f...  13.8 us
    dot_general x1, matrix products, on_device(): lax.dot_general(d_up, up_full, across, preferred_element_type=jnp.float32)  12.1 us
    dot_general x1, matrix products, on_device(): lax.dot_general(d_gate, gate_full, across, preferred_element_type=jnp.flo...  11.7 us
    another operation x1, other arithmetic  9.01 us
  transfers between devices with their start and end apart: 8, of which 6 were waited for; matrix products, arithmetic and copies ran while one was open for 31% of the time, Pallas kernels for 0%

profile of v1, /device:TPU:0, one launch (start us, length us, event | category | flops | bytes accessed | tf_op | source)
XLA Modules:
  0.0 348.9 jit_solution(5509503127290060144)
XLA Ops:
  7.2 0.0 all-gather.8.cloned.1.call-start
  7.2 0.7 all-gather.8.cloned.1.call-update
  7.9 0.0 copy-start.2
  7.9 0.0 copy-start.3
  7.9 0.0 all-gather.4.cloned.1.call-start
  8.0 0.7 all-gather.4.cloned.1.call-update
  8.7 0.0 all-gather.6.cloned.1.call-start
  8.7 0.7 all-gather.6.cloned.1.call-update
  9.4 1.8 fusion.12
  11.2 0.1 pad_maximum_fusion
  11.3 0.5 collective-permute-start
  11.9 17.9 %collective-permute-done = bf16[192,3584]{1,0:T(8,128)(2,1)S(1)} collective-permute-done((bf16[192,3584]{1,0:T(8,128)(2,1)S(1)}, bf16[192,3584]{1,0:T(8,128)(2,1)S(1)}, u32[]{:S(2)}, u32[]{:S(2)}) %collective-permute-start) | collective-permute-done | bytes 1376288 | tf_op jit(solution)/shard_map/ppermute | solution.py:41
  29.8 1.1 copy-done
  30.9 0.0 collective-permute-start.1
  30.9 17.8 %collective-permute-done.1 = bf16[192,3584]{1,0:T(8,128)(2,1)} collective-permute-done((bf16[192,3584]{1,0:T(8,128)(2,1)S(1)}, bf16[192,3584]{1,0:T(8,128)(2,1)}, u32[]{:S(2)}, u32[]{:S(2)}) %collective-permute-start.1) | collective-permute-done | bytes 1376288 | tf_op jit(solution)/shard_map/ppermute | solution.py:41
  48.7 0.0 collective-permute-start.2
  48.7 8.3 %all-gather.8.cloned.1.call-done = bf16[192,4096]{1,0:T(8,128)(2,1)} async-done(((bf16[24,4096]{1,0:T(8,128)(2,1)}), bf16[192,4096]{1,0:T(8,128)(2,1)}) %all-gather.8.cloned.1.call-update) | async-done | bytes 1572880 | tf_op jit(solution)/shard_map/all_gather | solution.py:8
  57.0 2.7 copy.12
  59.8 3.6 %all-to-all-start = ((bf16[192,4,1024]{2,0,1:T(8,128)(2,1)}), bf16[192,4,1024]{2,0,1:T(8,128)(2,1)S(1)}, u32[]{:S(2)}, u32[]{:S(2)}) async-start(bf16[192,4,1024]{2,0,1:T(8,128)(2,1)} %bitcast.12), calls=%async_computation.1 | async-start | bytes 3145728 | tf_op jit(solution)/shard_map/all_to_all | solution.py:35
  63.3 0.0 reduce-scatter.2.cloned.1.call-start
  63.4 0.0 copy-start.1
  63.4 3.4 collective-permute-done.2
  66.8 1.7 constant_dynamic-update-slice_fusion.7
  68.4 1.6 constant_dynamic-update-slice_fusion.6
  70.1 0.1 constant_dynamic-update-slice_fusion.5
  70.2 0.1 constant_dynamic-update-slice_fusion.4
  70.2 1.8 constant_dynamic-update-slice_fusion.3
  72.1 1.6 constant_dynamic-update-slice_fusion.2
  73.7 0.1 constant_dynamic-update-slice_fusion.1
  73.8 0.1 constant_dynamic-update-slice_fusion
  73.9 3.7 %constant_dynamic-slice_fusion = bf16[768,3584]{1,0:T(8,128)(2,1)} fusion(bf16[1536,3584]{1,0:T(8,128)(2,1)S(1)} %constant_dynamic-update-slice_fusion, s32[]{:T(128)S(6)} %select_n.22), kind=kLoop, calls=%fused_computation.30 | loop fusion | bytes 11010052 | tf_op jit(solution)/shard_map/jit(_roll_dynamic)/dynamic_slice | solution.py:44
  77.6 86.7 %all-gather.4.cloned.1.call-done = bf16[4096,1792]{1,0:T(8,128)(2,1)} async-done(((bf16[1024,1792]{1,0:T(8,128)(2,1)}), bf16[4096,1792]{1,0:T(8,128)(2,1)}) %all-gather.4.cloned.1.call-update) | async-done | bytes 14680080 | tf_op jit(solution)/shard_map/all_gather | solution.py:10
  164.2 11.7 %fusion.14 = f32[192,4096]{1,0:T(8,128)} fusion(bf16[192,1792]{1,0:T(8,128)(2,1)S(1)} %get-tuple-element.109, bf16[4096,1792]{1,0:T(8,128)(2,1)} %all-gather.4.cloned.1.call-done), kind=kOutput, calls=%fused_computation.32 | convolution fusion | flops 2818572288 | bytes 18513920 | tf_op jit(solution)/shard_map/dot_general | solution.py:25
  175.9 85.9 %all-gather.6.cloned.1.call-done = bf16[4096,1792]{1,0:T(8,128)(2,1)} async-done(((bf16[1024,1792]{1,0:T(8,128)(2,1)}), bf16[4096,1792]{1,0:T(8,128)(2,1)}) %all-gather.6.cloned.1.call-update) | async-done | bytes 14680080 | tf_op jit(solution)/shard_map/all_gather | solution.py:11
  261.9 12.1 %fusion.3 = bf16[192,4096]{1,0:T(8,128)(2,1)} fusion(f32[192,4096]{1,0:T(8,128)} %fusion.14, bf16[192,1792]{1,0:T(8,128)(2,1)S(1)} %get-tuple-element.108, bf16[4096,1792]{1,0:T(8,128)(2,1)} %all-gather.6.cloned.1.call-done), kind=kOutput, calls=%fused_computation.6 | convolution fusion | flops 2820145152 | bytes 20086784 | tf_op jit(solution)/shard_map/dot_general | solution.py:26
  274.0 0.0 reduce-scatter.2.cloned.1.call-update
  274.0 0.0 all-to-all-done
  274.0 52.6 %while.14 = (s32[]{:T(128)}, f32[1024,3584]{1,0:T(8,128)}, bf16[768,1024]{1,0:T(8,128)(2,1)S(1)}, bf16[768,3584]{1,0:T(8,128)(2,1)}, s32[]{:T(128)}, /*index=5*/s32[]{:T(128)}, s32[]{:T(128)}, s32[]{:T(128)}) while((s32[]{:T(128)}, f32[1024,3584]{1,0:T(8,128)}, bf16[768,1024]{1,0:T(8,128)(2,1)S(1)}, bf16[768,3584]{1,0:T(8,128)(2,1)}, ...), condition=%wide.region_2.3_spmd.clone, body=%wide.region_1.2_spmd.clone.sunk | while | flops 1423966208 | bytes 45810836 | solution.py:57
  274.0 3.5 convolution_convert_fusion.2
  277.5 5.9 %select_add_fusion.2 = f32[1024,3584]{1,0:T(8,128)} fusion(f32[1024,3584]{1,0:T(8,128)} %get-tuple-element.144, bf16[1024,3584]{1,0:T(8,128)(2,1)S(1)} %convolution_convert_fusion.2, pred[]{:T(512)S(6)} %compare.3), kind=kLoop, calls=%fused_computation.clone.1 | loop fusion | flops 11010048 | bytes 36700160 | tf_op jit(solution)/shard_map/while/body/eval_jaxpr/add | solution.py:55
  283.4 3.5 convolution_convert_fusion.2
  286.9 10.9 %select_add_fusion.2 = f32[1024,3584]{1,0:T(8,128)} fusion(f32[1024,3584]{1,0:T(8,128)} %get-tuple-element.144, bf16[1024,3584]{1,0:T(8,128)(2,1)S(1)} %convolution_convert_fusion.2, pred[]{:T(512)S(6)} %compare.3), kind=kLoop, calls=%fused_computation.clone.1 | loop fusion | flops 11010048 | bytes 36700160 | tf_op jit(solution)/shard_map/while/body/eval_jaxpr/add | solution.py:55
  297.8 3.5 convolution_convert_fusion.2
  301.2 11.0 %select_add_fusion.2 = f32[1024,3584]{1,0:T(8,128)} fusion(f32[1024,3584]{1,0:T(8,128)} %get-tuple-element.144, bf16[1024,3584]{1,0:T(8,128)(2,1)S(1)} %convolution_convert_fusion.2, pred[]{:T(512)S(6)} %compare.3), kind=kLoop, calls=%fused_computation.clone.1 | loop fusion | flops 11010048 | bytes 36700160 | tf_op jit(solution)/shard_map/while/body/eval_jaxpr/add | solution.py:55
  312.2 3.5 convolution_convert_fusion.2
  315.7 11.0 %select_add_fusion.2 = f32[1024,3584]{1,0:T(8,128)} fusion(f32[1024,3584]{1,0:T(8,128)} %get-tuple-element.144, bf16[1024,3584]{1,0:T(8,128)(2,1)S(1)} %convolution_convert_fusion.2, pred[]{:T(512)S(6)} %compare.3), kind=kLoop, calls=%fused_computation.clone.1 | loop fusion | flops 11010048 | bytes 36700160 | tf_op jit(solution)/shard_map/while/body/eval_jaxpr/add | solution.py:55
  326.6 9.0 %convert.4 = bf16[1024,3584]{1,0:T(8,128)(2,1)} convert(f32[1024,3584]{1,0:T(8,128)} %get-tuple-element.82) | non-fusion elementwise | flops 3670016 | bytes 22020096 | tf_op jit(solution)/shard_map/convert.1
  335.6 6.7 %fusion.13 = (bf16[1024,1792]{1,0:T(8,128)(2,1)}, bf16[1024,1792]{1,0:T(8,128)(2,1)}) fusion(bf16[1024,3584]{1,0:T(8,128)(2,1)} %convert.4), kind=kLoop, calls=%fused_computation.31 | loop fusion | bytes 14680064 | tf_op jit(solution)/shard_map/slice | solution.py:59
  (6 shorter events, 0.0 us)
Async XLA Ops:
  7.2 49.9 %all-gather.8.cloned.1.call-start = ((), (), s32[]{:S(2)}) async-start(), calls=%async_computation.5 | async-start | bytes 1769472 | tf_op jit(solution)/shard_map/all_gather | solution.py:8
  7.9 1.5 copy-start.2
  7.9 1.5 copy-start.3
  7.9 156.3 %all-gather.4.cloned.1.call-start = ((), (), s32[]{:S(2)}) async-start(), calls=%async_computation.2 | async-start | bytes 18350080 | tf_op jit(solution)/shard_map/all_gather | solution.py:10
  8.7 253.2 %all-gather.6.cloned.1.call-start = ((), (), s32[]{:S(2)}) async-start(), calls=%async_computation.3 | async-start | bytes 18350080 | tf_op jit(solution)/shard_map/all_gather | solution.py:11
  11.3 18.5 %collective-permute-start = (bf16[192,3584]{1,0:T(8,128)(2,1)S(1)}, bf16[192,3584]{1,0:T(8,128)(2,1)S(1)}, u32[]{:S(2)}, u32[]{:S(2)}) collective-permute-start(bf16[192,3584]{1,0:T(8,128)(2,1)S(1)} %pad_maximum_fusion), channel_id=1, source_target_pairs={{0,1},{1,2},{2,3},{3,0},{4,5},{5,6},{6,7},{7,4},{8,9},{9,10},{10,1... | collective-permute-start | bytes 4128776 | tf_op jit(solution)/shard_map/ppermute | solution.py:41
  29.8 1.1 copy-start
  30.9 17.8 %collective-permute-start.1 = (bf16[192,3584]{1,0:T(8,128)(2,1)S(1)}, bf16[192,3584]{1,0:T(8,128)(2,1)}, u32[]{:S(2)}, u32[]{:S(2)}) collective-permute-start(bf16[192,3584]{1,0:T(8,128)(2,1)S(1)} %collective-permute-done), channel_id=1, source_target_pairs={{0,1},{1,2},{2,3},{3,0},{4,5},{5,6},{6,7},{7,4},{8,9},{9,10},{10,1... | collective-permute-start | bytes 4128776 | tf_op jit(solution)/shard_map/ppermute | solution.py:41
  48.7 18.1 %collective-permute-start.2 = (bf16[192,3584]{1,0:T(8,128)(2,1)}, bf16[192,3584]{1,0:T(8,128)(2,1)}, u32[]{:S(2)}, u32[]{:S(2)}) collective-permute-start(bf16[192,3584]{1,0:T(8,128)(2,1)} %collective-permute-done.1), channel_id=1, source_target_pairs={{0,1},{1,2},{2,3},{3,0},{4,5},{5,6},{6,7},{7,4},{8,9},{9,10},{10,1... | collective-permute-start | bytes 4128776 | tf_op jit(solution)/shard_map/ppermute | solution.py:41
  59.8 214.3 %all-to-all-start = ((bf16[192,4,1024]{2,0,1:T(8,128)(2,1)}), bf16[192,4,1024]{2,0,1:T(8,128)(2,1)S(1)}, u32[]{:S(2)}, u32[]{:S(2)}) async-start(bf16[192,4,1024]{2,0,1:T(8,128)(2,1)} %bitcast.12), calls=%async_computation.1 | async-start | bytes 3145728 | tf_op jit(solution)/shard_map/all_to_all | solution.py:35
  63.3 279.0 %reduce-scatter.2.cloned.1.call-start = ((), (), s32[]{:S(2)}) async-start(), calls=%async_computation.4 | async-start | bytes 1769472 | tf_op jit(solution)/shard_map/reduce_scatter | solution.py:23
  63.4 6.7 %copy-start.1 = (bf16[192,3584]{1,0:T(8,128)(2,1)S(1)}, bf16[192,3584]{1,0:T(8,128)(2,1)}, u32[]{:S(2)}) copy-start(bf16[192,3584]{1,0:T(8,128)(2,1)} %copy-done) | copy-start | bytes 4128772
Sparse Core Ops, SparseCore 0:
  10.2 46.8 all-gather.7
  58.6 105.5 all-gather.3
  165.8 96.0 all-gather.5
  274.1 65.4 reduce-scatter.1
